TPU v7x, 32 devices: a whole 2x2x4 slice. The times are simulated.
32 devices in a mesh: gx: 4 (over z), gy: 8 (over y, x, core).
Axes of the slice: x: 2, y: 2, z: 4, core: 2. Of those that a mesh axis runs over, the one named last changes fastest.
Arguments:
- policy_logp: float32 [16, 512, 4096], P('gy', 'gx'), may hold values from -2 to 0
- anchor_logp: float32 [16, 512, 4096], P('gy', 'gx'), may hold values from -2 to 0
- lengths: int32 [16, 512], P('gy', 'gx'), may hold values from 512 to 4096
- rewards: int32 [16, 512], P('gy', 'gx'), may hold values from 0 to 8
- slot_prompt: int32 [16, 512], P('gy', 'gx'), may hold values from 0 to 511, as said below
Outputs:
- token_grad: float32 [16, 512, 4096], P(None, ('gx', 'gy'))
- sample_loss: float32 [16, 512], P(None, ('gx', 'gy'))
- advantage: float32 [16, 512], P(None, ('gx', 'gy'))
Inputs may be any that keep to these rules, and one draw needn't show every extreme that they name: `slot_prompt`: for every member k and every aligned block of 128 slots, the slots of the block hold each prompt of the same block exactly once.
All inputs are finite; a program needn't handle non-finite values.
Results may differ from a plain program's by a relative error of at most 0.00002.
Values sent between devices are 32-bit elements; how exact they have to be, the bound alone decides.
A program may use at most 64 MiB of HBM per device.

v0:
```python
import jax
import jax.numpy as jnp
from jax import lax
from jax.sharding import PartitionSpec as P

kl_weight = 0.1


def score_tokens(policy, anchor, seq_len, reward, total, members, grad_scale, loss_scale):
    advantage = (members * reward - total[None, :]) / (members - 1)
    positions = lax.broadcasted_iota(jnp.float32, policy.shape, 2)
    valid = positions < seq_len[:, :, None]
    log_ratio = anchor - policy
    ratio = jnp.exp(log_ratio)
    token_term = -advantage[:, :, None] * policy + kl_weight * (ratio - log_ratio - 1.0)
    token_grad = (
        jnp.where(valid, -advantage[:, :, None] + kl_weight * (1.0 - ratio), 0.0) * grad_scale
    )
    sample_loss = jnp.sum(jnp.where(valid, token_term, 0.0), axis=2) * loss_scale
    return (token_grad, sample_loss, advantage)


def body(policy_logp, anchor_logp, lengths, rewards, slot_prompt):
    members_dev, slots, seq_slots = policy_logp.shape
    local_prompt = slot_prompt % slots
    member_rows = lax.broadcasted_iota(jnp.int32, (members_dev, slots), 0)
    slot_ids = lax.broadcasted_iota(jnp.int32, (members_dev, slots), 1)
    inverse = jnp.zeros((members_dev, slots), jnp.int32).at[member_rows, local_prompt].set(slot_ids)
    sorted_policy = jnp.take_along_axis(policy_logp, inverse[:, :, None], axis=1)
    sorted_anchor = jnp.take_along_axis(anchor_logp, inverse[:, :, None], axis=1)
    sorted_len = jnp.take_along_axis(lengths, inverse, axis=1).astype(jnp.float32)
    sorted_reward = jnp.take_along_axis(rewards, inverse, axis=1).astype(jnp.float32) * 0.25
    count_local = jnp.sum(lengths.astype(jnp.float32))
    token_total = lax.psum(count_local, ("gx", "gy"))
    members = members_dev * lax.axis_size("gy")
    samples = members * slots * lax.axis_size("gx")
    grad_scale = samples * seq_slots / token_total
    loss_scale = samples / token_total
    member_sums = jnp.sum(sorted_reward, axis=0)
    total = lax.psum(member_sums, "gy")
    token_grad, sample_loss, advantage = score_tokens(
        sorted_policy,
        sorted_anchor,
        sorted_len,
        sorted_reward,
        total,
        members,
        grad_scale,
        loss_scale,
    )
    return (
        lax.all_to_all(token_grad, "gy", split_axis=1, concat_axis=0, tiled=True),
        lax.all_to_all(sample_loss, "gy", split_axis=1, concat_axis=0, tiled=True),
        lax.all_to_all(advantage, "gy", split_axis=1, concat_axis=0, tiled=True),
    )


def solution(mesh):
    placed = (P("gy", "gx", None), P("gy", "gx", None), P("gy", "gx"), P("gy", "gx"), P("gy", "gx"))
    return jax.shard_map(
        body,
        mesh=mesh,
        in_specs=placed,
        out_specs=(P(None, ("gx", "gy"), None), P(None, ("gx", "gy")), P(None, ("gx", "gy"))),
        check_vma=False,
    )
```

profile of v0, /device:TPU:0, one launch (start us, length us, event | category | flops | bytes accessed | tf_op | source)
XLA Modules:
  0.0 189.2 jit_solution(11175729835720736867)
XLA Ops:
  0.6 0.0 copy-start
  0.7 0.7 fusion.16
  1.4 11.4 %scatter_fusion = s32[2,128]{1,0:T(2,128)S(1)} fusion(s32[2,128]{1,0:T(2,128)S(1)} %broadcast.49, s32[256]{0:T(256)S(1)} %fusion.16, s32[256]{0:T(256)S(1)} %iota_bitcast_fusion), kind=kCustom, calls=%fused_computation.4 | custom fusion | bytes 5120 | tf_op jit(solution)/shard_map/scatter | solution.py:28
  12.8 1.3 convert_reduce_fusion
  14.1 2.3 %gather_fusion = s32[256]{0:T(256)S(1)} fusion(s32[2,128]{1,0:T(2,128)} %param.11, s32[256]{0:T(256)S(1)} %get-tuple-element.10), kind=kCustom, calls=%fused_computation.clone | custom fusion | bytes 4096 | tf_op jit(solution)/shard_map/jit(take_along_axis)/gather | solution.py:31
  16.5 0.0 copy-done
  16.5 2.4 %gather_fusion.1 = s32[256]{0:T(256)S(1)} fusion(s32[2,128]{1,0:T(2,128)S(1)} %copy-done, s32[256]{0:T(256)S(1)} %get-tuple-element.10), kind=kCustom, calls=%fused_computation.2.clone | custom fusion | bytes 4096 | tf_op jit(solution)/shard_map/jit(take_along_axis)/gather | solution.py:32
  18.9 15.1 %psum.14 = f32[128]{0:T(128)S(1)} all-reduce(f32[128]{0:T(128)S(1)} %multiply_reduce_fusion), channel_id=1, replica_groups=mesh['gx'=4,'gy'=8] {'gy'}, use_global_device_ids=true, to_apply=%region_2.4 | all-reduce | flops 128 | bytes 1024 | tf_op jit(solution)/shard_map/psum | solution.py:40
  34.1 0.1 copy.35
  34.2 0.1 copy.34
  34.3 7.6 %gather_fusion.2 = f32[256,4096]{1,0:T(8,128)} fusion(f32[2,128,4096]{2,1,0:T(8,128)} %param.10, s32[256]{0:T(256)S(1)} %get-tuple-element.9), kind=kCustom, calls=%fused_computation.1.clone | custom fusion | bytes 8390656 | tf_op jit(solution)/shard_map/jit(take_along_axis)/gather | solution.py:30
  41.9 7.6 %gather_fusion.3 = f32[256,4096]{1,0:T(8,128)} fusion(f32[2,128,4096]{2,1,0:T(8,128)} %param.9, s32[256]{0:T(256)S(1)} %get-tuple-element.9), kind=kCustom, calls=%fused_computation.3.clone | custom fusion | bytes 8390656 | tf_op jit(solution)/shard_map/jit(take_along_axis)/gather | solution.py:29
  49.5 0.1 copy.36
  49.7 39.9 %psum.15 = f32[]{:T(128)} all-reduce(f32[]{:T(128)} %convert_reduce_fusion), channel_id=1, replica_groups=mesh['gx'=4,'gy'=8] {'gx','gy'}, use_global_device_ids=true, to_apply=%region_4.7 | all-reduce | flops 1 | bytes 8 | tf_op jit(solution)/shard_map/psum | solution.py:34
  90.9 20.6 %fusion.9 = (f32[2,128]{0,1:T(8,128)S(1)}, f32[2,128,4096]{2,0,1:T(2,128)}) fusion(f32[2,128,4096]{2,1,0:T(8,128)} %bitcast.49, pred[2,128]{0,1:T(8,128)(4,1)S(1)} %copy.36, f32[2,128]{0,1:T(8,128)S(1)} %copy.35, f32[2,128]{0,1:T(8,128)S(1)} %copy.34, f32[2,128,4096]{2,1,0:T(8,128)} %bitcast.48, f32[]{:T(128)S(6)} %div.14), kind=kLoop, calls=%fused_computation.19 | loop fusion | flops 16776960 | bytes 12586244 | tf_op jit(solution)/shard_map/reduce_sum | solution.py:19
  111.5 0.7 copy.42
  112.2 3.8 %all-to-all-start.1 = ((f32[2,8,16]{2,0,1:T(2,128)}), f32[2,8,16]{2,0,1:T(2,128)S(1)}, u32[]{:S(2)}, u32[]{:S(2)}) async-start(f32[2,8,16]{2,0,1:T(2,128)} %copy.42), calls=%async_computation.1 | async-start | bytes 16384 | tf_op jit(solution)/shard_map/all_to_all | solution.py:53
  116.0 0.1 all_to_all.46
  116.1 4.6 %all-to-all-done.1 = f32[2,8,16]{2,0,1:T(2,128)S(1)} async-done(((f32[2,8,16]{2,0,1:T(2,128)}), f32[2,8,16]{2,0,1:T(2,128)S(1)}, u32[]{:S(2)}, u32[]{:S(2)}) %all-to-all-start.1) | async-done | bytes 1056 | tf_op jit(solution)/shard_map/all_to_all | solution.py:53
  120.7 7.1 %all_to_all.53 = f32[2,8,16]{2,0,1:T(2,128)S(1)} all-to-all(f32[2,8,16]{2,0,1:T(2,128)S(1)} %copy.43), channel_id=1, replica_groups=mesh['gx'=4,'gy'=8] {'gy'}, dimensions={1} | all-to-all | bytes 2048 | tf_op jit(solution)/shard_map/all_to_all | solution.py:54
  127.8 4.5 %all-to-all-start = ((f32[2,128,4096]{2,0,1:T(2,128)}), f32[2,128,4096]{2,0,1:T(2,128)}, u32[]{:S(2)}, u32[]{:S(2)}) async-start(f32[2,128,4096]{2,0,1:T(2,128)} %get-tuple-element.8), calls=%async_computation | async-start | bytes 8388608 | tf_op jit(solution)/shard_map/all_to_all | solution.py:52
  132.3 49.1 %all-to-all-done = f32[2,128,4096]{2,0,1:T(2,128)} async-done(((f32[2,128,4096]{2,0,1:T(2,128)}), f32[2,128,4096]{2,0,1:T(2,128)}, u32[]{:S(2)}, u32[]{:S(2)}) %all-to-all-start) | async-done | bytes 4194336 | tf_op jit(solution)/shard_map/all_to_all | solution.py:52
  181.4 6.6 %copy.40 = f32[8,2,16,4096]{3,2,1,0:T(8,128)} copy(f32[8,2,16,4096]{3,1,2,0:T(2,128)} %bitcast.13) | data formatting | bytes 8388608 | tf_op jit(solution)/shard_map/all_to_all | solution.py:52
  188.0 0.6 copy.66
  188.6 0.6 copy.67
  (9 shorter events, 0.1 us)
Async XLA Ops:
  0.6 15.8 %copy-start = (s32[2,128]{1,0:T(2,128)S(1)}, s32[2,128]{1,0:T(2,128)}, u32[]{:S(2)}) copy-start(s32[2,128]{1,0:T(2,128)} %param.12) | copy-start | bytes 3076
  112.2 8.5 %all-to-all-start.1 = ((f32[2,8,16]{2,0,1:T(2,128)}), f32[2,8,16]{2,0,1:T(2,128)S(1)}, u32[]{:S(2)}, u32[]{:S(2)}) async-start(f32[2,8,16]{2,0,1:T(2,128)} %copy.42), calls=%async_computation.1 | async-start | bytes 16384 | tf_op jit(solution)/shard_map/all_to_all | solution.py:53
  127.8 53.7 %all-to-all-start = ((f32[2,128,4096]{2,0,1:T(2,128)}), f32[2,128,4096]{2,0,1:T(2,128)}, u32[]{:S(2)}, u32[]{:S(2)}) async-start(f32[2,128,4096]{2,0,1:T(2,128)} %get-tuple-element.8), calls=%async_computation | async-start | bytes 8388608 | tf_op jit(solution)/shard_map/all_to_all | solution.py:52
where the time goes:
time: 190 us; the launch traced here: 189 us
  blocking collectives  62.1 us (33%)
  waiting for transfers between devices  53.7 us (28%)
  local copies, waits for them, and re-layouts  40.4 us (21%)
  other arithmetic  22.6 us (12%)
  starting transfers between devices  8.32 us (4%)
  between operations  2.09 us (1%)
    all_to_all x1, waiting for transfers between devices, body(): lax.all_to_all(token_grad, 'gy', split_axis=1, concat_axis=0, tiled=True)  49.1 us
    psum x1, blocking collectives, body(): token_total = lax.psum(count_local, ('gx', 'gy'))  39.9 us
    reduce_sum x1, other arithmetic, score_tokens(): jnp.sum(jnp.where(valid, token_term, 0.0), axis=2) * loss_scale  20.6 us
    psum x1, blocking collectives, body(): total = lax.psum(member_sums, 'gy')  15.1 us
    scatter x1, local copies, waits for them, and re-layouts, body(): jnp.zeros((members_dev, slots), jnp.int32).at[member_rows, local_prompt]  11.4 us
    gather x1, local copies, waits for them, and re-layouts, body(): jnp.take_along_axis(policy_logp, inverse[:, :, None], axis=1)  7.64 us
    gather x1, local copies, waits for them, and re-layouts, body(): jnp.take_along_axis(anchor_logp, inverse[:, :, None], axis=1)  7.59 us
    all_to_all x1, blocking collectives, body(): lax.all_to_all(advantage, 'gy', split_axis=1, concat_axis=0, tiled=True)  7.06 us
  transfers between devices with their start and end apart: 2, of which 2 were waited for; matrix products, arithmetic and copies ran while one was open for 0% of the time, Pallas kernels for 0%

commit v1 on v0

--- a/solution.py
+++ b/solution.py
@@ -37,7 +37,7 @@
     grad_scale = samples * seq_slots / token_total
     loss_scale = samples / token_total
     member_sums = jnp.sum(sorted_reward, axis=0)
-    total = lax.psum(member_sums, "gy")
+    total = jnp.sum(lax.all_gather(member_sums, "gy"), axis=0)
     token_grad, sample_loss, advantage = score_tokens(
         sorted_policy,
         sorted_anchor,

time: 190 us -> 186 us (0.979)
  blocking collectives: 62.1 us -> 57.2 us
    psum x1 -> x0, blocking collectives: 15.1 us -> none  [body(): total = lax.psum(member_sums, 'gy')]
    all_gather x0 -> x1, blocking collectives: none -> 10.3 us  [body(): total = jnp.sum(lax.all_gather(member_sums, 'gy'), axis=0)]
where the time goes in v1:
time: 186 us; the launch traced here: 185 us
  blocking collectives  57.2 us (31%)
  waiting for transfers between devices  53.7 us (29%)
  local copies, waits for them, and re-layouts  40.4 us (22%)
  other arithmetic  22.6 us (12%)
  starting transfers between devices  9.31 us (5%)
  between operations  2.09 us (1%)
    all_to_all x1, waiting for transfers between devices, body(): lax.all_to_all(token_grad, 'gy', split_axis=1, concat_axis=0, tiled=True)  49.1 us
    psum x1, blocking collectives, body(): token_total = lax.psum(count_local, ('gx', 'gy'))  39.9 us
    reduce_sum x1, other arithmetic, score_tokens(): jnp.sum(jnp.where(valid, token_term, 0.0), axis=2) * loss_scale  20.6 us
    scatter x1, local copies, waits for them, and re-layouts, body(): jnp.zeros((members_dev, slots), jnp.int32).at[member_rows, local_prompt]  11.4 us
    all_gather x1, blocking collectives, body(): total = jnp.sum(lax.all_gather(member_sums, 'gy'), axis=0)  10.3 us
    gather x1, local copies, waits for them, and re-layouts, body(): jnp.take_along_axis(policy_logp, inverse[:, :, None], axis=1)  7.64 us
    gather x1, local copies, waits for them, and re-layouts, body(): jnp.take_along_axis(anchor_logp, inverse[:, :, None], axis=1)  7.59 us
    all_to_all x1, blocking collectives, body(): lax.all_to_all(advantage, 'gy', split_axis=1, concat_axis=0, tiled=True)  7.06 us
  transfers between devices with their start and end apart: 2, of which 2 were waited for; matrix products, arithmetic and copies ran while one was open for 0% of the time, Pallas kernels for 0%

profile of v1, /device:TPU:0, one launch (start us, length us, event | category | flops | bytes accessed | tf_op | source)
XLA Modules:
  0.0 185.3 jit_solution(11010620639445221697)
XLA Ops:
  0.6 0.0 copy-start
  0.7 0.7 fusion.16
  1.4 11.4 %scatter_fusion = s32[2,128]{1,0:T(2,128)S(1)} fusion(s32[2,128]{1,0:T(2,128)S(1)} %broadcast.49, s32[256]{0:T(256)S(1)} %fusion.16, s32[256]{0:T(256)S(1)} %iota_bitcast_fusion), kind=kCustom, calls=%fused_computation.4 | custom fusion | bytes 5120 | tf_op jit(solution)/shard_map/scatter | solution.py:28
  12.8 1.3 convert_reduce_fusion
  14.1 2.3 %gather_fusion = s32[256]{0:T(256)S(1)} fusion(s32[2,128]{1,0:T(2,128)} %param.11, s32[256]{0:T(256)S(1)} %get-tuple-element.10), kind=kCustom, calls=%fused_computation.clone | custom fusion | bytes 4096 | tf_op jit(solution)/shard_map/jit(take_along_axis)/gather | solution.py:31
  16.5 0.0 copy-done
  16.5 2.4 %gather_fusion.1 = s32[256]{0:T(256)S(1)} fusion(s32[2,128]{1,0:T(2,128)S(1)} %copy-done, s32[256]{0:T(256)S(1)} %get-tuple-element.10), kind=kCustom, calls=%fused_computation.2.clone | custom fusion | bytes 4096 | tf_op jit(solution)/shard_map/jit(take_along_axis)/gather | solution.py:32
  18.9 10.3 %all-gather.1 = f32[8,1,128]{2,1,0:T(1,128)S(1)} all-gather(f32[1,1,128]{2,1,0:T(1,128)S(1)} %bitcast.55), channel_id=2, replica_groups=mesh['gx'=4,'gy'=8] {'gy'}, dimensions={0}, use_global_device_ids=true | all-gather | bytes 4608 | tf_op jit(solution)/shard_map/all_gather | solution.py:40
  29.2 0.1 copy.35
  29.4 0.1 copy.34
  29.5 7.6 %gather_fusion.2 = f32[256,4096]{1,0:T(8,128)} fusion(f32[2,128,4096]{2,1,0:T(8,128)} %param.10, s32[256]{0:T(256)S(1)} %get-tuple-element.9), kind=kCustom, calls=%fused_computation.1.clone | custom fusion | bytes 8390656 | tf_op jit(solution)/shard_map/jit(take_along_axis)/gather | solution.py:30
  37.1 7.6 %gather_fusion.3 = f32[256,4096]{1,0:T(8,128)} fusion(f32[2,128,4096]{2,1,0:T(8,128)} %param.9, s32[256]{0:T(256)S(1)} %get-tuple-element.9), kind=kCustom, calls=%fused_computation.3.clone | custom fusion | bytes 8390656 | tf_op jit(solution)/shard_map/jit(take_along_axis)/gather | solution.py:29
  44.7 0.1 copy.36
  44.8 39.9 %psum.7 = f32[]{:T(128)} all-reduce(f32[]{:T(128)} %convert_reduce_fusion), channel_id=1, replica_groups=mesh['gx'=4,'gy'=8] {'gx','gy'}, use_global_device_ids=true, to_apply=%region_4.7 | all-reduce | flops 1 | bytes 8 | tf_op jit(solution)/shard_map/psum | solution.py:34
  86.1 20.6 %fusion.9 = (f32[2,128]{0,1:T(8,128)S(1)}, f32[2,128,4096]{2,0,1:T(2,128)}) fusion(f32[2,128,4096]{2,1,0:T(8,128)} %bitcast.50, pred[2,128]{0,1:T(8,128)(4,1)S(1)} %copy.36, f32[2,128]{0,1:T(8,128)S(1)} %copy.35, f32[2,128]{0,1:T(8,128)S(1)} %copy.34, f32[2,128,4096]{2,1,0:T(8,128)} %bitcast.49, f32[]{:T(128)S(6)} %div.14), kind=kLoop, calls=%fused_computation.19 | loop fusion | flops 16776960 | bytes 12586244 | tf_op jit(solution)/shard_map/reduce_sum | solution.py:19
  106.6 0.7 copy.42
  107.4 4.8 %all-to-all-start.1 = ((f32[2,8,16]{2,0,1:T(2,128)}), f32[2,8,16]{2,0,1:T(2,128)S(1)}, u32[]{:S(2)}, u32[]{:S(2)}) async-start(f32[2,8,16]{2,0,1:T(2,128)} %copy.42), calls=%async_computation.1 | async-start | bytes 16384 | tf_op jit(solution)/shard_map/all_to_all | solution.py:53
  112.1 0.1 all_to_all.46
  112.2 4.6 %all-to-all-done.1 = f32[2,8,16]{2,0,1:T(2,128)S(1)} async-done(((f32[2,8,16]{2,0,1:T(2,128)}), f32[2,8,16]{2,0,1:T(2,128)S(1)}, u32[]{:S(2)}, u32[]{:S(2)}) %all-to-all-start.1) | async-done | bytes 1056 | tf_op jit(solution)/shard_map/all_to_all | solution.py:53
  116.8 7.1 %all_to_all.53 = f32[2,8,16]{2,0,1:T(2,128)S(1)} all-to-all(f32[2,8,16]{2,0,1:T(2,128)S(1)} %copy.43), channel_id=1, replica_groups=mesh['gx'=4,'gy'=8] {'gy'}, dimensions={1} | all-to-all | bytes 2048 | tf_op jit(solution)/shard_map/all_to_all | solution.py:54
  123.9 4.5 %all-to-all-start = ((f32[2,128,4096]{2,0,1:T(2,128)}), f32[2,128,4096]{2,0,1:T(2,128)}, u32[]{:S(2)}, u32[]{:S(2)}) async-start(f32[2,128,4096]{2,0,1:T(2,128)} %get-tuple-element.8), calls=%async_computation | async-start | bytes 8388608 | tf_op jit(solution)/shard_map/all_to_all | solution.py:52
  128.5 49.1 %all-to-all-done = f32[2,128,4096]{2,0,1:T(2,128)} async-done(((f32[2,128,4096]{2,0,1:T(2,128)}), f32[2,128,4096]{2,0,1:T(2,128)}, u32[]{:S(2)}, u32[]{:S(2)}) %all-to-all-start) | async-done | bytes 4194336 | tf_op jit(solution)/shard_map/all_to_all | solution.py:52
  177.5 6.6 %copy.40 = f32[8,2,16,4096]{3,2,1,0:T(8,128)} copy(f32[8,2,16,4096]{3,1,2,0:T(2,128)} %bitcast.14) | data formatting | bytes 8388608 | tf_op jit(solution)/shard_map/all_to_all | solution.py:52
  184.1 0.6 copy.66
  184.7 0.6 copy.67
  (10 shorter events, 0.1 us)
Async XLA Ops:
  0.6 15.8 %copy-start = (s32[2,128]{1,0:T(2,128)S(1)}, s32[2,128]{1,0:T(2,128)}, u32[]{:S(2)}) copy-start(s32[2,128]{1,0:T(2,128)} %param.12) | copy-start | bytes 3076
  107.4 9.5 %all-to-all-start.1 = ((f32[2,8,16]{2,0,1:T(2,128)}), f32[2,8,16]{2,0,1:T(2,128)S(1)}, u32[]{:S(2)}, u32[]{:S(2)}) async-start(f32[2,8,16]{2,0,1:T(2,128)} %copy.42), calls=%async_computation.1 | async-start | bytes 16384 | tf_op jit(solution)/shard_map/all_to_all | solution.py:53
  123.9 53.7 %all-to-all-start = ((f32[2,128,4096]{2,0,1:T(2,128)}), f32[2,128,4096]{2,0,1:T(2,128)}, u32[]{:S(2)}, u32[]{:S(2)}) async-start(f32[2,128,4096]{2,0,1:T(2,128)} %get-tuple-element.8), calls=%async_computation | async-start | bytes 8388608 | tf_op jit(solution)/shard_map/all_to_all | solution.py:52
